TPU v7x, 32 devices: a whole 2x2x4 slice. The times are simulated.
32 devices in a mesh: band: 8 (over z, x), ga: 4 (over y, core).
Axes of the slice: x: 2, y: 2, z: 4, core: 2. Of those that a mesh axis runs over, the one named last changes fastest.
Arguments:
- elements: bfloat16 [2, 768, 2048], P(None, 'band', 'ga'), may hold values from -0.75 to 0.75
- screened: bfloat16 [2, 2, 2048, 2048], P(None, None, 'ga'), may hold values from -0.09375 to 0.09375
- energies: float32 [768], replicated, may hold values from -3 to 3
- freq_points: float32 [2], replicated, may hold values from -3 to 3
- freq_weights: float32 [2], replicated, may hold values from 0.5 to 2
- band_of_slot: int32 [768], replicated, may hold values from 0 to 767, each once
Outputs:
- sigma: float32 [2, 768, 768], P(None, 'band', 'ga')
Inputs may be any that keep to these rules, and one draw needn't show every extreme that they name: `band_of_slot`: each of 0 to 767 stands once.
All inputs are finite; a program needn't handle non-finite values.
Results may differ from a plain program's by a relative error of at most 0.0042.
Values may be sent and summed in bfloat16 or wider, within the bound.
No kernel may reach another device: no remote copies, remote signals or barrier semaphores. Data moves between devices by JAX's collectives and lax.ppermute only.
A program may use at most 128 MiB of HBM per device.

v0:
```python
import jax
import jax.numpy as jnp
from jax import lax
from jax.sharding import PartitionSpec as P


def make_left(block):
    flipped = jnp.stack([-block[1], block[0]])
    return jnp.stack([block, flipped])


def on_device(elements, screened, energies, freq_points, freq_weights, band_of_slot):
    bands = elements.shape[1]
    slot_energy = jnp.take(energies, band_of_slot)
    offset = slot_energy[None, :] - freq_points[:, None]
    screen = freq_weights[:, None] / (1.0 + 4.0 * offset * offset)
    own_start = lax.axis_index("band") * bands
    screen_own = lax.dynamic_slice_in_dim(screen, own_start, bands, 1)
    piece = lax.all_gather(elements, "ga", axis=2, tiled=True)
    real_side = jnp.stack([piece[0], -piece[1]])
    imag_side = jnp.stack([piece[1], piece[0]])
    sides = jnp.stack([real_side, imag_side])
    applied = jnp.einsum(
        "dcmk,wcgk->wdmg", sides, screened, preferred_element_type=jnp.float32
    ).astype(jnp.bfloat16)
    left_own = make_left(elements)
    pairs = jnp.einsum(
        "dcnk,wcmk->wdnm",
        left_own,
        lax.all_gather(applied, "band", axis=2, tiled=True),
        preferred_element_type=jnp.float32,
    )
    factor = 0.5 * (screen_own[:, :, None] + screen[:, None, :])
    partial_rows = jnp.sum(pairs * factor[:, None], axis=0)
    return lax.psum_scatter(partial_rows, "ga", scatter_dimension=2, tiled=True)


def solution(mesh):
    placed = (P(None, "band", "ga"), P(None, None, "ga", None), P(), P(), P(), P())
    return jax.shard_map(
        on_device, mesh=mesh, in_specs=placed, out_specs=P(None, "band", "ga"), check_vma=False
    )
```

profile of v0, /device:TPU:0, one launch (start us, length us, event | category | flops | bytes accessed | tf_op | source)
XLA Modules:
  0.0 121.1 jit_solution(2113868990376874802)
XLA Ops:
  6.5 0.0 copy-start
  6.5 0.0 all-gather.2.cloned.1.call-start
  6.5 10.4 %all_gather.6 = bf16[2,96,2048]{2,1,0:T(8,128)(2,1)S(1)} all-gather(bf16[2,96,512]{2,1,0:T(8,128)(2,1)} %param.6), channel_id=1, replica_groups=mesh['band'=8,'ga'=4] {'ga'}, dimensions={2}, use_global_device_ids=true | all-gather | bytes 983040 | tf_op jit(solution)/shard_map/all_gather | solution.py:19
  17.0 0.1 slice_negate_fusion.1
  17.1 0.1 maximum_bitcast_fusion.8
  17.2 0.0 copy-start.2
  17.2 7.0 %fusion.21 = bf16[2,2,96,512]{3,2,1,0:T(8,128)(2,1)} fusion(bf16[2,2,512,2048]{3,2,1,0:T(8,128)(2,1)} %param.7, bf16[1,2,96,2048]{3,2,1,0:T(8,128)(2,1)S(1)} %get-tuple-element.9, bf16[1,2,96,2048]{3,2,1,0:T(8,128)(2,1)S(1)} %get-tuple-element.8), kind=kOutput, calls=%fused_computation.13 | convolution fusion | flops 1613955072 | bytes 10354688 | tf_op jit(solution)/shard_map/dcmk,wcgk->wdmg/dot_general | solution.py:23
  24.2 0.0 copy-start.3
  24.2 0.0 copy-start.4
  24.2 0.0 copy-start.1
  24.2 0.0 all-gather.2.cloned.1.call-update
  24.3 0.0 reduce-scatter.4.cloned.1.call-start
  24.3 0.0 copy-done.2
  24.4 0.0 copy-done
  24.4 3.2 %gather_fusion = f32[768]{0:T(1024)S(1)} fusion(f32[768]{0:T(1024)S(1)} %copy-done, s32[1024]{0:T(1024)S(1)} %pad_clamp_fusion), kind=kCustom, calls=%fused_computation | custom fusion | bytes 9216 | tf_op jit(solution)/shard_map/jit(_take)/gather | solution.py:14
  27.6 0.0 copy-done.3
  27.6 0.0 copy-done.4
  27.6 0.1 fusion.27
  27.7 0.1 constant_dynamic-slice_fusion
  27.8 0.0 copy-done.1
  27.8 0.1 add_multiply_fusion
  27.9 57.3 %all-gather.2.cloned.1.call-done = bf16[2,2,768,512]{3,2,1,0:T(8,128)(2,1)} async-done(((bf16[2,2,96,512]{3,2,1,0:T(8,128)(2,1)}), bf16[2,2,768,512]{3,2,1,0:T(8,128)(2,1)}) %all-gather.2.cloned.1.call-update) | async-done | bytes 3145744 | tf_op jit(solution)/shard_map/all_gather | solution.py:30
  85.3 3.1 %fusion.12 = f32[2,96,768]{2,1,0:T(8,128)S(1)} fusion(bf16[2,2,768,512]{3,2,1,0:T(8,128)(2,1)} %all-gather.2.cloned.1.call-done, f32[2,96,768]{2,1,0:T(8,128)S(1)} %add_multiply_fusion, bf16[1,2,96,512]{3,2,1,0:T(8,128)(2,1)S(1)} %maximum_bitcast_fusion.12, bf16[1,2,96,512]{3,2,1,0:T(8,128)(2,1)S(1)} %bitcast.63), kind=kOutput, calls=%fused_computation.10 | convolution fusion | flops 605208576 | bytes 4718592 | tf_op jit(solution)/shard_map/dcnk,wcmk->wdnm/dot_general | solution.py:27
  88.4 0.5 copy.11
  88.9 1.4 %reshape.63 = f32[768,192]{1,0:T(8,128)} reshape(f32[768,2,96]{2,1,0:T(2,128)S(1)} %bitcast.61) | data formatting | bytes 1179648
  90.2 0.0 reduce-scatter.4.cloned.1.call-update
  90.3 22.0 %reduce-scatter.4.cloned.1.call-done = f32[192,192]{1,0:T(8,128)} async-done(((f32[768,192]{1,0:T(8,128)}), f32[192,192]{1,0:T(8,128)}) %reduce-scatter.4.cloned.1.call-update) | async-done | bytes 147472
  112.3 1.1 reshape.64
  113.4 0.8 copy.12
  (5 shorter events, 0.1 us)
Async XLA Ops:
  6.5 17.8 %copy-start = (f32[768]{0:T(1024)S(1)}, f32[768]{0:T(1024)}, u32[]{:S(2)}) copy-start(f32[768]{0:T(1024)} %param.8) | copy-start | bytes 9220
  6.5 78.7 %all-gather.2.cloned.1.call-start = ((), (), s32[]{:S(2)}) async-start(), calls=%async_computation.1 | async-start | bytes 3538944 | tf_op jit(solution)/shard_map/all_gather | solution.py:30
  17.2 7.1 %copy-start.2 = (s32[768]{0:T(1024)S(1)}, s32[768]{0:T(1024)}, u32[]{:S(2)}) copy-start(s32[768]{0:T(1024)} %param.11) | copy-start | bytes 9220
  24.2 3.3 %copy-start.3 = (f32[2]{0:T(128)S(1)}, f32[2]{0:T(128)}, u32[]{:S(2)}) copy-start(f32[2]{0:T(128)} %param.10) | copy-start | bytes 28
  24.2 3.4 %copy-start.4 = (f32[2]{0:T(128)S(1)}, f32[2]{0:T(128)}, u32[]{:S(2)}) copy-start(f32[2]{0:T(128)} %param.9) | copy-start | bytes 28
  24.2 3.5 %copy-start.1 = (bf16[2,96,512]{2,1,0:T(8,128)(2,1)S(1)}, bf16[2,96,512]{2,1,0:T(8,128)(2,1)}, u32[]{:S(2)}) copy-start(bf16[2,96,512]{2,1,0:T(8,128)(2,1)} %param.6) | copy-start | bytes 589828
  24.3 88.0 %reduce-scatter.4.cloned.1.call-start = ((), (), s32[]{:S(2)}) async-start(), calls=%async_computation.2 | async-start | bytes 983040
Sparse Core Ops, SparseCore 0:
  24.4 60.8 all-gather.1
  90.4 21.8 reduce-scatter.3
where the time goes:
time: 121 us
  waiting for transfers between devices  79.4 us (66%)
  between operations  13.5 us (11%)
  blocking collectives  10.4 us (9%)
  matrix products  10.2 us (8%)
  local copies, waits for them, and re-layouts  7.04 us (6%)
    all_gather x1, waiting for transfers between devices, on_device(): lax.all_gather(applied, 'band', axis=2, tiled=True)  57.3 us
    unnamed x3, waiting for transfers between devices  22.1 us
    all_gather x1, blocking collectives, on_device(): piece = lax.all_gather(elements, 'ga', axis=2, tiled=True)  10.4 us
    dot_general x1, matrix products, on_device(): jnp.einsum('dcmk,wcgk->wdmg', sides, screened, preferred_element_type=jnp...  7.03 us
    unnamed x14, local copies, waits for them, and re-layouts  3.77 us
    gather x1, local copies, waits for them, and re-layouts, on_device(): slot_energy = jnp.take(energies, band_of_slot)  3.19 us
    dot_general x1, matrix products, on_device(): jnp.einsum('dcnk,wcmk->wdnm', left_own, lax.all_gather(applied, 'band', a...  3.12 us
  transfers between devices with their start and end apart: 2, of which 2 were waited for; matrix products, arithmetic and copies ran while one was open for 3% of the time, Pallas kernels for 0%

commit v1 on v0

--- a/solution.py
+++ b/solution.py
@@ -2,6 +2,21 @@
 import jax.numpy as jnp
 from jax import lax
 from jax.sharding import PartitionSpec as P
+
+
+def on_each_block(value, axis, dim, make, out_dim):
+    ways, here, lap = (lax.axis_size(axis), lax.axis_index(axis), value.shape[dim])
+    results = []
+    for far in range(ways):
+        arriving = (
+            lax.ppermute(value, axis, [(d, (d + 1) % ways) for d in range(ways)])
+            if far + 1 < ways
+            else value
+        )
+        results.append(make(value, (here - far) % ways * lap))
+        value = arriving
+    line = jnp.concatenate(results[::-1], axis=out_dim)
+    return jnp.roll(line, (here + 1) * results[0].shape[out_dim], axis=out_dim)
 
 
 def make_left(block):
@@ -24,11 +39,14 @@
         "dcmk,wcgk->wdmg", sides, screened, preferred_element_type=jnp.float32
     ).astype(jnp.bfloat16)
     left_own = make_left(elements)
-    pairs = jnp.einsum(
-        "dcnk,wcmk->wdnm",
-        left_own,
-        lax.all_gather(applied, "band", axis=2, tiled=True),
-        preferred_element_type=jnp.float32,
+    pairs = on_each_block(
+        applied,
+        "band",
+        2,
+        lambda shard, start: jnp.einsum(
+            "dcnk,wcmk->wdnm", left_own, shard, preferred_element_type=jnp.float32
+        ),
+        3,
     )
     factor = 0.5 * (screen_own[:, :, None] + screen[:, None, :])
     partial_rows = jnp.sum(pairs * factor[:, None], axis=0)

time: 121 us -> 143 us (1.18)
  waiting for transfers between devices: 79.4 us -> 93.4 us
  local copies, waits for them, and re-layouts: 7.04 us -> 10.2 us
  matrix products: 10.2 us -> 12.1 us
  starting transfers between devices: 0.04 us -> 1.57 us
    ppermute x0 -> x7, waiting for transfers between devices: none -> 73.2 us  [on_each_block(): lax.ppermute(value, axis, [(d, (d + 1) % ways) for d in range(ways)])]
    all_gather x1 -> x0, waiting for transfers between devices: 57.3 us -> none  [on_device(): lax.all_gather(applied, 'band', axis=2, tiled=True)]
    concatenate x0 -> x1, local copies, waits for them, and re-layouts: none -> 3.15 us  [on_each_block(): return jnp.roll(line, (here + 1) * results[0].shape[out_dim], axis=out_dim)]
    dot_general x1 -> x8, matrix products: 3.12 us -> 5.87 us  [on_device(): jnp.einsum('dcnk,wcmk->wdnm', left_own, shard, preferred_element_type=jnp...]
    unnamed x3 -> x2, waiting for transfers between devices: 22.1 us -> 20.3 us
    ppermute x0 -> x7, starting transfers between devices: none -> 1.57 us  [on_each_block(): lax.ppermute(value, axis, [(d, (d + 1) % ways) for d in range(ways)])]
    unnamed x14 -> x18, local copies, waits for them, and re-layouts: 3.77 us -> 3.81 us
  transfers between devices with their start and end apart: 2 -> 8, of which waited for: 2 -> 8; matrix products, arithmetic and copies ran while one was open for 3% -> 6% of each run, Pallas kernels for 0% -> 0%
where the time goes in v1:
time: 143 us; the launch traced here: 142 us
  waiting for transfers between devices  93.4 us (65%)
  between operations  13.6 us (10%)
  matrix products  12.1 us (8%)
  blocking collectives  10.4 us (7%)
  local copies, waits for them, and re-layouts  10.2 us (7%)
  starting transfers between devices  1.57 us (1%)
    ppermute x7, waiting for transfers between devices, on_each_block(): lax.ppermute(value, axis, [(d, (d + 1) % ways) for d in range(ways)])  73.2 us
    unnamed x2, waiting for transfers between devices  20.3 us
    all_gather x1, blocking collectives, on_device(): piece = lax.all_gather(elements, 'ga', axis=2, tiled=True)  10.4 us
    dot_general x1, matrix products, on_device(): jnp.einsum('dcmk,wcgk->wdmg', sides, screened, preferred_element_type=jnp...  6.28 us
    dot_general x8, matrix products, on_device(): jnp.einsum('dcnk,wcmk->wdnm', left_own, shard, preferred_element_type=jnp...  5.87 us
    unnamed x18, local copies, waits for them, and re-layouts  3.81 us
    gather x1, local copies, waits for them, and re-layouts, on_device(): slot_energy = jnp.take(energies, band_of_slot)  3.19 us
    concatenate x1, local copies, waits for them, and re-layouts, on_each_block(): return jnp.roll(line, (here + 1) * results[0].shape[out_dim], axis=out_dim)  3.15 us
  transfers between devices with their start and end apart: 8, of which 8 were waited for; matrix products, arithmetic and copies ran while one was open for 6% of the time, Pallas kernels for 0%

profile of v1, /device:TPU:0, one launch (start us, length us, event | category | flops | bytes accessed | tf_op | source)
XLA Modules:
  0.0 142.2 jit_solution(1200504000061221668)
XLA Ops:
  6.5 10.4 %all_gather.3 = bf16[2,96,2048]{2,1,0:T(8,128)(2,1)S(1)} all-gather(bf16[2,96,512]{2,1,0:T(8,128)(2,1)} %param.6), channel_id=1, replica_groups=mesh['band'=8,'ga'=4] {'ga'}, dimensions={2}, use_global_device_ids=true | all-gather | bytes 983040 | tf_op jit(solution)/shard_map/all_gather | solution.py:34
  17.0 0.1 slice_negate_fusion.1
  17.1 0.1 maximum_bitcast_fusion.6
  17.2 6.3 %fusion.7 = bf16[2,96,2,512]{3,1,2,0:T(8,128)(2,1)S(1)} fusion(bf16[2,2,512,2048]{3,2,1,0:T(8,128)(2,1)} %param.7, bf16[1,2,96,2048]{3,2,1,0:T(8,128)(2,1)S(1)} %get-tuple-element.9, bf16[1,2,96,2048]{3,2,1,0:T(8,128)(2,1)S(1)} %get-tuple-element.8), kind=kOutput, calls=%fused_computation.7 | convolution fusion | flops 1613955072 | bytes 10354688 | tf_op jit(solution)/shard_map/dcmk,wcgk->wdmg/dot_general | solution.py:38
  23.5 1.6 %collective-permute-start = (bf16[2,2,96,512]{3,2,0,1:T(8,128)(2,1)S(1)}, bf16[2,2,96,512]{3,2,0,1:T(8,128)(2,1)S(1)}, u32[]{:S(2)}, u32[]{:S(2)}) collective-permute-start(bf16[2,2,96,512]{3,2,0,1:T(8,128)(2,1)S(1)} %bitcast.124), channel_id=1, source_target_pairs={{0,4},{4,8},{8,12},{12,16},{16,20},{20,24},{24,28},{28,0},{1,5},{5... | collective-permute-start | bytes 1179656 | tf_op jit(solution)/shard_map/ppermute | solution.py:12
  25.1 12.7 %collective-permute-done = bf16[2,2,96,512]{3,2,0,1:T(8,128)(2,1)S(1)} collective-permute-done((bf16[2,2,96,512]{3,2,0,1:T(8,128)(2,1)S(1)}, bf16[2,2,96,512]{3,2,0,1:T(8,128)(2,1)S(1)}, u32[]{:S(2)}, u32[]{:S(2)}) %collective-permute-start) | collective-permute-done | bytes 393248 | tf_op jit(solution)/shard_map/ppermute | solution.py:12
  37.8 3.2 %gather_fusion = f32[768]{0:T(1024)S(1)} fusion(f32[768]{0:T(1024)S(1)} %copy-done, s32[1024]{0:T(1024)S(1)} %pad_clamp_fusion), kind=kCustom, calls=%fused_computation | custom fusion | bytes 9216 | tf_op jit(solution)/shard_map/jit(_take)/gather | solution.py:29
  41.0 10.1 %collective-permute-done.1 = bf16[2,2,96,512]{3,2,0,1:T(8,128)(2,1)S(1)} collective-permute-done((bf16[2,2,96,512]{3,2,0,1:T(8,128)(2,1)S(1)}, bf16[2,2,96,512]{3,2,0,1:T(8,128)(2,1)S(1)}, u32[]{:S(2)}, u32[]{:S(2)}) %collective-permute-start.1) | collective-permute-done | bytes 393248 | tf_op jit(solution)/shard_map/ppermute | solution.py:12
  51.1 0.1 fusion.19
  51.2 12.3 %collective-permute-done.2 = bf16[2,2,96,512]{3,2,0,1:T(8,128)(2,1)S(1)} collective-permute-done((bf16[2,2,96,512]{3,2,0,1:T(8,128)(2,1)S(1)}, bf16[2,2,96,512]{3,2,0,1:T(8,128)(2,1)S(1)}, u32[]{:S(2)}, u32[]{:S(2)}) %collective-permute-start.2) | collective-permute-done | bytes 393248 | tf_op jit(solution)/shard_map/ppermute | solution.py:12
  63.5 0.1 constant_dynamic-slice_fusion
  63.6 11.5 %collective-permute-done.3 = bf16[2,2,96,512]{3,2,0,1:T(8,128)(2,1)S(1)} collective-permute-done((bf16[2,2,96,512]{3,2,0,1:T(8,128)(2,1)S(1)}, bf16[2,2,96,512]{3,2,0,1:T(8,128)(2,1)S(1)}, u32[]{:S(2)}, u32[]{:S(2)}) %collective-permute-start.3) | collective-permute-done | bytes 393248 | tf_op jit(solution)/shard_map/ppermute | solution.py:12
  75.1 0.3 convolution_bitcast_fusion
  75.4 0.1 add_multiply_fusion
  75.5 10.3 %collective-permute-done.4 = bf16[2,2,96,512]{3,2,0,1:T(8,128)(2,1)S(1)} collective-permute-done((bf16[2,2,96,512]{3,2,0,1:T(8,128)(2,1)S(1)}, bf16[2,2,96,512]{3,2,0,1:T(8,128)(2,1)S(1)}, u32[]{:S(2)}, u32[]{:S(2)}) %collective-permute-start.4) | collective-permute-done | bytes 393248 | tf_op jit(solution)/shard_map/ppermute | solution.py:12
  85.8 0.3 convolution_bitcast_fusion.1
  86.1 0.3 convolution_bitcast_fusion.2
  86.5 1.0 convolution_bitcast_fusion.3
  87.4 8.9 %collective-permute-done.5 = bf16[2,2,96,512]{3,2,0,1:T(8,128)(2,1)S(1)} collective-permute-done((bf16[2,2,96,512]{3,2,0,1:T(8,128)(2,1)S(1)}, bf16[2,2,96,512]{3,2,0,1:T(8,128)(2,1)S(1)}, u32[]{:S(2)}, u32[]{:S(2)}) %collective-permute-start.5) | collective-permute-done | bytes 393248 | tf_op jit(solution)/shard_map/ppermute | solution.py:12
  96.3 1.0 convolution_bitcast_fusion.4
  97.3 1.0 convolution_bitcast_fusion.5
  98.3 1.0 convolution_bitcast_fusion.6
  99.3 7.5 %collective-permute-done.6 = bf16[2,2,96,512]{3,2,0,1:T(8,128)(2,1)S(1)} collective-permute-done((bf16[2,2,96,512]{3,2,0,1:T(8,128)(2,1)S(1)}, bf16[2,2,96,512]{3,2,0,1:T(8,128)(2,1)S(1)}, u32[]{:S(2)}, u32[]{:S(2)}) %collective-permute-start.6) | collective-permute-done | bytes 393248 | tf_op jit(solution)/shard_map/ppermute | solution.py:12
  106.8 1.0 convolution_bitcast_fusion.7
  107.8 3.1 %concatenate.6 = f32[2,2,96,1536]{3,2,1,0:T(8,128)S(1)} concatenate(f32[2,2,96,96]{3,2,1,0:T(8,128)} %convolution_bitcast_fusion.7, f32[2,2,96,96]{3,2,1,0:T(8,128)} %convolution_bitcast_fusion.6, f32[2,2,96,96]{3,2,1,0:T(8,128)} %convolution_bitcast_fusion.5, f32[2,2,96,96]{3,2,1,0:T(8,128)} %convolution_bitcast_fusion.4, f32[2,2,96,96]{3,2,1,0:T(8,128)} %convolution_bitcast_fusion.3, ...), dimensions={3} | concatenate | bytes 4718592 | tf_op jit(solution)/shard_map/jit(_roll_dynamic)/concatenate | solution.py:19
  110.9 0.4 multiply_reduce_fusion
  111.3 0.5 copy.65
  111.8 1.4 reshape.77
  113.2 0.0 reduce-scatter.4.cloned.1.call-update
  113.2 20.3 %reduce-scatter.4.cloned.1.call-done = f32[192,192]{1,0:T(8,128)} async-done(((f32[768,192]{1,0:T(8,128)}), f32[192,192]{1,0:T(8,128)}) %reduce-scatter.4.cloned.1.call-update) | async-done | bytes 147472
  133.4 1.1 reshape.78
  134.5 0.8 copy.66
  (26 shorter events, 0.1 us)
Async XLA Ops:
  6.5 31.2 %copy-start = (f32[768]{0:T(1024)S(1)}, f32[768]{0:T(1024)}, u32[]{:S(2)}) copy-start(f32[768]{0:T(1024)} %param.8) | copy-start | bytes 9220
  6.5 126.9 %reduce-scatter.4.cloned.1.call-start = ((), (), s32[]{:S(2)}) async-start(), calls=%async_computation.1 | async-start | bytes 983040
  17.2 20.6 %copy-start.2 = (s32[768]{0:T(1024)S(1)}, s32[768]{0:T(1024)}, u32[]{:S(2)}) copy-start(s32[768]{0:T(1024)} %param.11) | copy-start | bytes 9220
  23.5 27.6 %copy-start.3 = (f32[2]{0:T(128)S(1)}, f32[2]{0:T(128)}, u32[]{:S(2)}) copy-start(f32[2]{0:T(128)} %param.10) | copy-start | bytes 28
  23.5 27.6 %copy-start.4 = (f32[2]{0:T(128)S(1)}, f32[2]{0:T(128)}, u32[]{:S(2)}) copy-start(f32[2]{0:T(128)} %param.9) | copy-start | bytes 28
  23.5 40.0 %copy-start.1 = (bf16[2,96,512]{2,1,0:T(8,128)(2,1)S(1)}, bf16[2,96,512]{2,1,0:T(8,128)(2,1)}, u32[]{:S(2)}) copy-start(bf16[2,96,512]{2,1,0:T(8,128)(2,1)} %param.6) | copy-start | bytes 589828
  23.5 14.2 %collective-permute-start = (bf16[2,2,96,512]{3,2,0,1:T(8,128)(2,1)S(1)}, bf16[2,2,96,512]{3,2,0,1:T(8,128)(2,1)S(1)}, u32[]{:S(2)}, u32[]{:S(2)}) collective-permute-start(bf16[2,2,96,512]{3,2,0,1:T(8,128)(2,1)S(1)} %bitcast.124), channel_id=1, source_target_pairs={{0,4},{4,8},{8,12},{12,16},{16,20},{20,24},{24,28},{28,0},{1,5},{5... | collective-permute-start | bytes 1179656 | tf_op jit(solution)/shard_map/ppermute | solution.py:12
  37.7 13.3 %collective-permute-start.1 = (bf16[2,2,96,512]{3,2,0,1:T(8,128)(2,1)S(1)}, bf16[2,2,96,512]{3,2,0,1:T(8,128)(2,1)S(1)}, u32[]{:S(2)}, u32[]{:S(2)}) collective-permute-start(bf16[2,2,96,512]{3,2,0,1:T(8,128)(2,1)S(1)} %collective-permute-done), channel_id=1, source_target_pairs={{0,4},{4,8},{8,12},{12,16},{16,20},{20,24},{24,28},{28,0},{1,5},{5... | collective-permute-start | bytes 1179656 | tf_op jit(solution)/shard_map/ppermute | solution.py:12
  51.0 12.4 %collective-permute-start.2 = (bf16[2,2,96,512]{3,2,0,1:T(8,128)(2,1)S(1)}, bf16[2,2,96,512]{3,2,0,1:T(8,128)(2,1)S(1)}, u32[]{:S(2)}, u32[]{:S(2)}) collective-permute-start(bf16[2,2,96,512]{3,2,0,1:T(8,128)(2,1)S(1)} %collective-permute-done.1), channel_id=1, source_target_pairs={{0,4},{4,8},{8,12},{12,16},{16,20},{20,24},{24,28},{28,0},{1,5},{5... | collective-permute-start | bytes 1179656 | tf_op jit(solution)/shard_map/ppermute | solution.py:12
  63.5 11.6 %collective-permute-start.3 = (bf16[2,2,96,512]{3,2,0,1:T(8,128)(2,1)S(1)}, bf16[2,2,96,512]{3,2,0,1:T(8,128)(2,1)S(1)}, u32[]{:S(2)}, u32[]{:S(2)}) collective-permute-start(bf16[2,2,96,512]{3,2,0,1:T(8,128)(2,1)S(1)} %collective-permute-done.2), channel_id=1, source_target_pairs={{0,4},{4,8},{8,12},{12,16},{16,20},{20,24},{24,28},{28,0},{1,5},{5... | collective-permute-start | bytes 1179656 | tf_op jit(solution)/shard_map/ppermute | solution.py:12
  75.1 10.7 %copy-start.5 = (bf16[2,2,96,512]{3,2,0,1:T(8,128)(2,1)}, bf16[2,2,96,512]{3,2,0,1:T(8,128)(2,1)S(1)}, u32[]{:S(2)}) copy-start(bf16[2,2,96,512]{3,2,0,1:T(8,128)(2,1)S(1)} %collective-permute-done.3) | copy-start | bytes 1179652
  75.1 10.7 %collective-permute-start.4 = (bf16[2,2,96,512]{3,2,0,1:T(8,128)(2,1)S(1)}, bf16[2,2,96,512]{3,2,0,1:T(8,128)(2,1)S(1)}, u32[]{:S(2)}, u32[]{:S(2)}) collective-permute-start(bf16[2,2,96,512]{3,2,0,1:T(8,128)(2,1)S(1)} %collective-permute-done.3), channel_id=1, source_target_pairs={{0,4},{4,8},{8,12},{12,16},{16,20},{20,24},{24,28},{28,0},{1,5},{5... | collective-permute-start | bytes 1179656 | tf_op jit(solution)/shard_map/ppermute | solution.py:12
  85.8 10.5 %collective-permute-start.5 = (bf16[2,2,96,512]{3,2,0,1:T(8,128)(2,1)S(1)}, bf16[2,2,96,512]{3,2,0,1:T(8,128)(2,1)S(1)}, u32[]{:S(2)}, u32[]{:S(2)}) collective-permute-start(bf16[2,2,96,512]{3,2,0,1:T(8,128)(2,1)S(1)} %collective-permute-done.4), channel_id=1, source_target_pairs={{0,4},{4,8},{8,12},{12,16},{16,20},{20,24},{24,28},{28,0},{1,5},{5... | collective-permute-start | bytes 1179656 | tf_op jit(solution)/shard_map/ppermute | solution.py:12
  85.8 10.5 %copy-start.6 = (bf16[2,2,96,512]{3,2,0,1:T(8,128)(2,1)S(1)}, bf16[2,2,96,512]{3,2,0,1:T(8,128)(2,1)}, u32[]{:S(2)}) copy-start(bf16[2,2,96,512]{3,2,0,1:T(8,128)(2,1)} %copy-done.5) | copy-start | bytes 1179652
  96.3 10.5 %collective-permute-start.6 = (bf16[2,2,96,512]{3,2,0,1:T(8,128)(2,1)S(1)}, bf16[2,2,96,512]{3,2,0,1:T(8,128)(2,1)S(1)}, u32[]{:S(2)}, u32[]{:S(2)}) collective-permute-start(bf16[2,2,96,512]{3,2,0,1:T(8,128)(2,1)S(1)} %collective-permute-done.5), channel_id=1, source_target_pairs={{0,4},{4,8},{8,12},{12,16},{16,20},{20,24},{24,28},{28,0},{1,5},{5... | collective-permute-start | bytes 1179656 | tf_op jit(solution)/shard_map/ppermute | solution.py:12
Sparse Core Ops, SparseCore 0:
  113.3 20.0 reduce-scatter.3
